TPU v7x, 512 devices: a whole 4x4x16 slice. The times are simulated.
512 devices in a mesh: tm: 16 (over z_lo, x), chan: 32 (over z_hi, y, core).
Axes of the slice: x: 4, y: 4, z: 16 (z_hi: 4, z_lo: 4; z = z_hi * 4 + z_lo), core: 2. Of those that a mesh axis runs over, the one named last changes fastest.
Arguments:
- voltages: bfloat16 [2, 128, 2048, 1024], P(None, 'tm', 'chan'), may hold values from -6 to 6
- subspace: float32 [32, 64, 32, 1024], P('chan', 'tm'), may hold values from -0.1875 to 0.1875
- order: int32 [64], replicated, may hold values from 0 to 63, each once
- beam_seeds: int32 [256], replicated, may hold values from 1 to 65520
- flagged: int32 [16], replicated, may hold values from 0 to 511
Outputs:
- beams: bfloat16 [2, 32, 64, 512, 128], P(None, None, 'tm', 'chan')
- tracked: float32 [32, 64, 32, 1024], P('chan', 'tm')
Inputs may be any that keep to these rules, and one draw needn't show every extreme that they name: `order`: each of 0 to 63 once. `flagged`: station numbers; a station may occur more than once.
All inputs are finite; a program needn't handle non-finite values.
Results may differ from a plain program's by a relative error of at most 0.0084.
Values may be sent and summed in bfloat16 or wider, within the bound.
No kernel may reach another device: no remote copies, remote signals or barrier semaphores. Data moves between devices by JAX's collectives and lax.ppermute only.
A program may use at most 64 MiB of HBM per device.

v0:
```python
import math
import jax
import jax.numpy as jnp
from jax import lax
from jax.sharding import PartitionSpec as P

CH = 2048
SUB = 2
TWO_PI = 2.0 * math.pi


def beam_weights(beam_seeds, channels, stations, total_channels):
    station_no = jnp.arange(stations, dtype=jnp.int32) + 1
    delays = (station_no[:, None] * beam_seeds[None, :] % 65521).astype(jnp.float32) / 65521.0
    frequency = 1.0 + channels.astype(jnp.float32) / total_channels
    angles = delays[None, :, :] * (TWO_PI * frequency)[:, None, None]
    factor = 1.0 / math.sqrt(stations)
    cosine = jnp.cos(angles) * factor
    sine_part = jnp.sin(angles) * factor
    upper = jnp.concatenate([cosine, sine_part], axis=2)
    under = jnp.concatenate([-sine_part, cosine], axis=2)
    return jnp.concatenate([upper, under], axis=1).astype(jnp.bfloat16)


def power_step(voltage_input, tracked, steering_weight):
    sample_count = voltage_input.shape[0]
    coarse_channel = tracked.astype(jnp.bfloat16)
    projected_input = jnp.einsum(
        "xbj,bqj->bxq", voltage_input, coarse_channel, preferred_element_type=jnp.float32
    ).astype(jnp.bfloat16)
    beam_image = (
        jnp.einsum(
            "nwg,wny->ngy", projected_input, voltage_input, preferred_element_type=jnp.float32
        )
        + sample_count * tracked
    )
    gram = jnp.einsum("crs,cks->crk", beam_image, beam_image, precision=lax.Precision.HIGHEST)
    lower = jnp.linalg.cholesky(gram)
    tracked = jax.scipy.linalg.solve_triangular(lower, beam_image, lower=True)
    subspace_vectors = tracked.astype(jnp.bfloat16)
    lengthwise_axis = jnp.einsum(
        "xbj,bqj->bxq", voltage_input, subspace_vectors, preferred_element_type=jnp.float32
    ).astype(jnp.bfloat16)
    mixing = jnp.einsum(
        "crs,csb->crb", subspace_vectors, steering_weight, preferred_element_type=jnp.float32
    ).astype(jnp.bfloat16)
    direct_output = jnp.einsum(
        "edi,diy->dye", voltage_input, steering_weight, preferred_element_type=jnp.float32
    )
    beams = direct_output - jnp.einsum(
        "ctr,crb->cbt", lengthwise_axis, mixing, preferred_element_type=jnp.float32
    )
    return (tracked, beams.astype(jnp.bfloat16))


def per_device(voltages, subspace, order, beam_seeds, flagged):
    signals = voltages.shape[-1]
    stations = signals // 2
    slots = subspace.shape[1]
    per_group = order.shape[0]
    marks = jnp.any(flagged[:, None] == jnp.arange(stations, dtype=jnp.int32)[None, :], axis=0)
    keep = jnp.where(marks, 0.0, 1.0).astype(jnp.bfloat16)
    keep = jnp.concatenate([keep, keep])
    ordered = jnp.take(voltages, order, axis=2) * keep
    group = lax.axis_index("chan")
    first_slot = lax.axis_index("tm") * slots
    chosen = lax.dynamic_slice_in_dim(order, first_slot, slots)
    channels = group * per_group + chosen
    steering_weight = beam_weights(beam_seeds, channels, stations, CH)
    state = subspace[0]
    results = []
    for part in range(SUB):
        turned = lax.all_to_all(ordered[part], "tm", split_axis=1, concat_axis=0, tiled=True)
        state, formed = power_step(turned, state, steering_weight)
        results.append(
            lax.all_to_all(formed[None], "chan", split_axis=2, concat_axis=0, tiled=True)
        )
    output = jnp.stack(results)
    return (output, state[None])


def solution(mesh):
    return jax.shard_map(
        per_device,
        mesh=mesh,
        in_specs=(P(None, "tm", "chan", None), P("chan", "tm", None, None), P(), P(), P()),
        out_specs=(P(None, None, "tm", "chan", None), P("chan", "tm", None, None)),
        check_vma=False,
    )
```

profile of v0, /device:TPU:12, one launch (start us, length us, event | category | flops | bytes accessed | tf_op | source)
XLA Modules:
  0.0 212.0 jit_solution(4434291030982119377)
XLA Ops:
  2.9 7.9 %gather_fusion = bf16[64,2,8,1024]{3,0,2,1:T(8,128)(2,1)} fusion(bf16[2,8,64,1024]{3,2,1,0:T(8,128)(2,1)S(1)} %copy-done, s32[1024]{0:T(1024)S(1)} %pad_clamp_fusion), kind=kCustom, calls=%fused_computation | custom fusion | bytes 4194560 | tf_op jit(solution)/shard_map/jit(_take)/gather | solution.py:64
  10.8 1.8 multiply_bitcast_fusion
  12.7 1.1 slice_bitcast_fusion.1
  13.8 1.5 copy.37
  15.4 8.9 %all-to-all-start = ((bf16[8,64,1024]{2,0,1:T(8,128)(2,1)}), bf16[8,64,1024]{2,0,1:T(8,128)(2,1)S(1)}, u32[]{:S(2)}, u32[]{:S(2)}) async-start(bf16[8,64,1024]{2,0,1:T(8,128)(2,1)} %copy.37), calls=%async_computation | async-start | bytes 2097152 | tf_op jit(solution)/shard_map/all_to_all | solution.py:73
  24.3 2.8 %copy.44 = bf16[8,64,1024]{2,0,1:T(8,128)(2,1)} copy(bf16[8,64,1024]{2,1,0:T(8,128)(2,1)} %get-tuple-element.5) | data formatting | bytes 2097152 | tf_op jit(solution)/shard_map/squeeze | solution.py:73
  27.1 21.2 %all-to-all-done = bf16[8,64,1024]{2,0,1:T(8,128)(2,1)S(1)} async-done(((bf16[8,64,1024]{2,0,1:T(8,128)(2,1)}), bf16[8,64,1024]{2,0,1:T(8,128)(2,1)S(1)}, u32[]{:S(2)}, u32[]{:S(2)}) %all-to-all-start) | async-done | bytes 1048608 | tf_op jit(solution)/shard_map/all_to_all | solution.py:73
  49.2 6.9 %all-to-all-start.2 = ((bf16[8,64,1024]{2,0,1:T(8,128)(2,1)}), bf16[8,64,1024]{2,0,1:T(8,128)(2,1)S(1)}, u32[]{:S(2)}, u32[]{:S(2)}) async-start(bf16[8,64,1024]{2,0,1:T(8,128)(2,1)} %copy.44), calls=%async_computation.2 | async-start | bytes 2097152 | tf_op jit(solution)/shard_map/all_to_all | solution.py:73
  56.6 9.1 %fusion.4 = (bf16[4,512,256]{1,2,0:T(8,128)(2,1)}, bf16[4,512,256]{1,2,0:T(8,128)(2,1)}, bf16[4,512,256]{1,2,0:T(8,128)(2,1)}) fusion(f32[4]{0:T(128)S(1)} %add_multiply_fusion, f32[512,256]{0,1:T(8,128)S(1)} %fusion.33), kind=kLoop, calls=%fused_computation.8 | loop fusion | flops 3670016 | bytes 3670032 | tf_op jit(solution)/shard_map/convert.5
  65.7 3.3 %convolution_add_fusion.1 = f32[4,32,1024]{2,1,0:T(8,128)} fusion(bf16[8,16,4,1024]{3,0,2,1:T(8,128)(2,1)} %bitcast.82, f32[1,4,32,1024]{3,2,1,0:T(8,128)} %param.9), kind=kOutput, calls=%fused_computation.18 | convolution fusion | flops 67518464 | bytes 2097152 | tf_op jit(solution)/shard_map/nwg,wny->ngy/dot_general | solution.py:32
  69.0 1.8 fusion.56
  71.0 11.7 %custom-call.8 = f32[4,32,32]{2,1,0:T(8,128)S(1)} custom-call(f32[4,32,32]{2,1,0:T(8,128)S(1)} %fusion.49), custom_call_target="Cholesky" | custom-call | tf_op jit(solution)/shard_map/jit(cholesky)/cholesky | solution.py:38
  82.9 9.8 %custom-call.9 = f32[4,1,32,32]{2,3,1,0:T(8,128)S(1)} custom-call(f32[4,1,32,32]{3,2,1,0:T(8,128)S(1)} %select_bitcast_fusion.1), custom_call_target="InvertDiagBlocksLowerTriangular" | custom-call | tf_op jit(solution)/shard_map/jit(_solve_triangular)/vmap()/triangular_solve | solution.py:39
  92.8 1.7 fusion.47
  95.3 3.7 %convolution_convert_fusion.1 = bf16[4,32,512]{2,1,0:T(8,128)(2,1)S(1)} fusion(f32[4,32,1024]{2,1,0:T(8,128)S(1)} %fusion.47, bf16[4,512,256]{1,2,0:T(8,128)(2,1)} %get-tuple-element.8, bf16[4,512,256]{1,2,0:T(8,128)(2,1)} %get-tuple-element.7, bf16[4,512,256]{1,2,0:T(8,128)(2,1)} %get-tuple-element.6), kind=kOutput, calls=%fused_computation.20 | convolution fusion | flops 151191552 | bytes 3801088 | tf_op jit(solution)/shard_map/crs,csb->crb/dot_general | solution.py:44
  99.0 2.2 %fusion.20 = f32[4,512,128]{2,1,0:T(8,128)} fusion(bf16[8,16,4,1024]{3,0,2,1:T(8,128)(2,1)S(1)} %bitcast.84, bf16[4,512,256]{1,2,0:T(8,128)(2,1)S(1)} %copy-done.9, bf16[4,512,256]{1,2,0:T(8,128)(2,1)S(1)} %copy-done.7, bf16[4,512,256]{1,2,0:T(8,128)(2,1)S(1)} %copy-done.5), kind=kOutput, calls=%fused_computation.34 | convolution fusion | flops 553648128 | bytes 5242880 | tf_op jit(solution)/shard_map/edi,diy->dye/dot_general | solution.py:47
  101.2 3.2 %fusion.9 = bf16[1,4,512,128]{3,2,1,0:T(8,128)(2,1)} fusion(f32[4,512,128]{2,1,0:T(8,128)} %fusion.20, bf16[4,32,512]{2,1,0:T(8,128)(2,1)S(1)} %convolution_convert_fusion.1, bf16[8,16,4,1024]{3,0,2,1:T(8,128)(2,1)} %bitcast.83, f32[4,32,1024]{2,1,0:T(8,128)} %copy-done.3), kind=kOutput, calls=%fused_computation.16 | convolution fusion | flops 51003392 | bytes 3276800 | tf_op jit(solution)/shard_map/ctr,crb->cbt/dot_general | solution.py:50
  104.5 2.2 %copy.42 = bf16[1,4,512,128]{3,1,0,2:T(4,128)(2,1)} copy(bf16[1,4,512,128]{3,2,1,0:T(8,128)(2,1)} %fusion.9) | data formatting | bytes 1048576 | tf_op jit(solution)/shard_map/broadcast_in_dim | solution.py:76
  106.7 15.7 %all-to-all-start.1 = ((bf16[1,4,512,128]{3,1,0,2:T(4,128)(2,1)}), bf16[1,4,512,128]{3,1,0,2:T(4,128)(2,1)}, u32[]{:S(2)}, u32[]{:S(2)}) async-start(bf16[1,4,512,128]{3,1,0,2:T(4,128)(2,1)} %copy.42), calls=%async_computation.1 | async-start | bytes 1048576 | tf_op jit(solution)/shard_map/all_to_all | solution.py:76
  122.4 2.7 %convolution_add_fusion = f32[4,32,1024]{2,1,0:T(8,128)} fusion(bf16[8,16,4,1024]{3,0,2,1:T(8,128)(2,1)S(1)} %bitcast.79, f32[4,32,1024]{2,1,0:T(8,128)} %copy-done.3), kind=kOutput, calls=%fused_computation.17 | convolution fusion | flops 67518464 | bytes 2097152 | tf_op jit(solution)/shard_map/nwg,wny->ngy/dot_general | solution.py:32
  125.1 1.8 fusion.57
  127.1 11.7 %custom-call.10 = f32[4,32,32]{2,1,0:T(8,128)S(1)} custom-call(f32[4,32,32]{2,1,0:T(8,128)S(1)} %fusion.46), custom_call_target="Cholesky" | custom-call | tf_op jit(solution)/shard_map/jit(cholesky)/cholesky | solution.py:38
  139.0 9.8 %custom-call.11 = f32[4,1,32,32]{2,3,1,0:T(8,128)S(1)} custom-call(f32[4,1,32,32]{3,2,1,0:T(8,128)S(1)} %select_bitcast_fusion), custom_call_target="InvertDiagBlocksLowerTriangular" | custom-call | tf_op jit(solution)/shard_map/jit(_solve_triangular)/vmap()/triangular_solve | solution.py:39
  148.9 1.7 fusion.44
  151.4 3.7 %convolution_convert_fusion = bf16[4,32,512]{2,1,0:T(8,128)(2,1)S(1)} fusion(f32[4,32,1024]{2,1,0:T(8,128)S(1)} %fusion.44, bf16[4,512,256]{1,2,0:T(8,128)(2,1)} %get-tuple-element.8, bf16[4,512,256]{1,2,0:T(8,128)(2,1)} %get-tuple-element.7, bf16[4,512,256]{1,2,0:T(8,128)(2,1)} %get-tuple-element.6), kind=kOutput, calls=%fused_computation.19 | convolution fusion | flops 151191552 | bytes 3801088 | tf_op jit(solution)/shard_map/crs,csb->crb/dot_general | solution.py:44
  155.1 2.3 %fusion.14 = f32[4,512,128]{2,1,0:T(8,128)} fusion(bf16[8,16,4,1024]{3,0,2,1:T(8,128)(2,1)S(1)} %bitcast.80, bf16[4,512,256]{1,2,0:T(8,128)(2,1)S(1)} %copy-done.10, bf16[4,512,256]{1,2,0:T(8,128)(2,1)S(1)} %copy-done.8, bf16[4,512,256]{1,2,0:T(8,128)(2,1)S(1)} %copy-done.6), kind=kOutput, calls=%fused_computation.30 | convolution fusion | flops 553648128 | bytes 5242880 | tf_op jit(solution)/shard_map/edi,diy->dye/dot_general | solution.py:47
  157.4 2.9 %fusion.8 = bf16[1,4,512,128]{3,2,1,0:T(8,128)(2,1)} fusion(f32[4,512,128]{2,1,0:T(8,128)} %fusion.14, bf16[4,32,512]{2,1,0:T(8,128)(2,1)S(1)} %convolution_convert_fusion, bf16[8,16,4,1024]{3,0,2,1:T(8,128)(2,1)S(1)} %bitcast.81, f32[4,32,1024]{2,1,0:T(8,128)} %copy-done.4), kind=kOutput, calls=%fused_computation.15 | convolution fusion | flops 51003392 | bytes 3276800 | tf_op jit(solution)/shard_map/ctr,crb->cbt/dot_general | solution.py:50
  160.3 2.2 %copy.49 = bf16[1,4,512,128]{3,1,0,2:T(4,128)(2,1)} copy(bf16[1,4,512,128]{3,2,1,0:T(8,128)(2,1)} %fusion.8) | data formatting | bytes 1048576 | tf_op jit(solution)/shard_map/broadcast_in_dim | solution.py:76
  162.5 14.6 %all-to-all-start.3 = ((bf16[1,4,512,128]{3,1,0,2:T(4,128)(2,1)}), bf16[1,4,512,128]{3,1,0,2:T(4,128)(2,1)S(1)}, u32[]{:S(2)}, u32[]{:S(2)}) async-start(bf16[1,4,512,128]{3,1,0,2:T(4,128)(2,1)} %copy.49), calls=%async_computation.3 | async-start | bytes 1048576 | tf_op jit(solution)/shard_map/all_to_all | solution.py:76
  177.1 1.1 copy.90
  178.2 32.6 %all-to-all-done.3 = bf16[1,4,512,128]{3,1,0,2:T(4,128)(2,1)S(1)} async-done(((bf16[1,4,512,128]{3,1,0,2:T(4,128)(2,1)}), bf16[1,4,512,128]{3,1,0,2:T(4,128)(2,1)S(1)}, u32[]{:S(2)}, u32[]{:S(2)}) %all-to-all-start.3) | async-done | bytes 524320 | tf_op jit(solution)/shard_map/all_to_all | solution.py:76
  210.9 1.1 pad_maximum_fusion
  (50 shorter events, 6.1 us)
Async XLA Ops:
  0.6 2.3 %copy-start = (bf16[2,8,64,1024]{3,2,1,0:T(8,128)(2,1)S(1)}, bf16[2,8,64,1024]{3,2,1,0:T(8,128)(2,1)}, u32[]{:S(2)}) copy-start(bf16[2,8,64,1024]{3,2,1,0:T(8,128)(2,1)} %param.8) | copy-start | bytes 6291460
  15.4 32.9 %all-to-all-start = ((bf16[8,64,1024]{2,0,1:T(8,128)(2,1)}), bf16[8,64,1024]{2,0,1:T(8,128)(2,1)S(1)}, u32[]{:S(2)}, u32[]{:S(2)}) async-start(bf16[8,64,1024]{2,0,1:T(8,128)(2,1)} %copy.37), calls=%async_computation | async-start | bytes 2097152 | tf_op jit(solution)/shard_map/all_to_all | solution.py:73
  24.2 31.9 %copy-start.12 = (s32[64]{0:T(128)S(1)}, s32[64]{0:T(128)}, u32[]{:S(2)}) copy-start(s32[64]{0:T(128)} %param.10) | copy-start | bytes 772
  24.3 32.0 %copy-start.11 = (s32[256]{0:T(256)S(1)}, s32[256]{0:T(256)}, u32[]{:S(2)}) copy-start(s32[256]{0:T(256)} %param.11) | copy-start | bytes 3076
  48.3 1.0 copy-start.1
  49.2 57.5 %all-to-all-start.2 = ((bf16[8,64,1024]{2,0,1:T(8,128)(2,1)}), bf16[8,64,1024]{2,0,1:T(8,128)(2,1)S(1)}, u32[]{:S(2)}, u32[]{:S(2)}) async-start(bf16[8,64,1024]{2,0,1:T(8,128)(2,1)} %copy.44), calls=%async_computation.2 | async-start | bytes 2097152 | tf_op jit(solution)/shard_map/all_to_all | solution.py:73
  94.5 0.8 copy-start.3
  95.3 3.7 %copy-start.2 = (bf16[8,64,1024]{2,0,1:T(8,128)(2,1)S(1)}, bf16[8,64,1024]{2,0,1:T(8,128)(2,1)}, u32[]{:S(2)}) copy-start(bf16[8,64,1024]{2,0,1:T(8,128)(2,1)} %copy-done.1) | copy-start | bytes 3145732
  95.3 3.7 %copy-start.5 = (bf16[4,512,256]{1,2,0:T(8,128)(2,1)S(1)}, bf16[4,512,256]{1,2,0:T(8,128)(2,1)}, u32[]{:S(2)}) copy-start(bf16[4,512,256]{1,2,0:T(8,128)(2,1)} %get-tuple-element.6) | copy-start | bytes 3145732
  95.3 3.7 %copy-start.7 = (bf16[4,512,256]{1,2,0:T(8,128)(2,1)S(1)}, bf16[4,512,256]{1,2,0:T(8,128)(2,1)}, u32[]{:S(2)}) copy-start(bf16[4,512,256]{1,2,0:T(8,128)(2,1)} %get-tuple-element.7) | copy-start | bytes 3145732
  95.3 3.7 %copy-start.9 = (bf16[4,512,256]{1,2,0:T(8,128)(2,1)S(1)}, bf16[4,512,256]{1,2,0:T(8,128)(2,1)}, u32[]{:S(2)}) copy-start(bf16[4,512,256]{1,2,0:T(8,128)(2,1)} %get-tuple-element.8) | copy-start | bytes 3145732
  106.7 55.8 %all-to-all-start.1 = ((bf16[1,4,512,128]{3,1,0,2:T(4,128)(2,1)}), bf16[1,4,512,128]{3,1,0,2:T(4,128)(2,1)}, u32[]{:S(2)}, u32[]{:S(2)}) async-start(bf16[1,4,512,128]{3,1,0,2:T(4,128)(2,1)} %copy.42), calls=%async_computation.1 | async-start | bytes 1048576 | tf_op jit(solution)/shard_map/all_to_all | solution.py:76
  150.6 0.8 copy-start.4
  151.4 3.7 %copy-start.6 = (bf16[4,512,256]{1,2,0:T(8,128)(2,1)S(1)}, bf16[4,512,256]{1,2,0:T(8,128)(2,1)}, u32[]{:S(2)}) copy-start(bf16[4,512,256]{1,2,0:T(8,128)(2,1)} %get-tuple-element.6) | copy-start | bytes 3145732
  151.4 3.7 %copy-start.8 = (bf16[4,512,256]{1,2,0:T(8,128)(2,1)S(1)}, bf16[4,512,256]{1,2,0:T(8,128)(2,1)}, u32[]{:S(2)}) copy-start(bf16[4,512,256]{1,2,0:T(8,128)(2,1)} %get-tuple-element.7) | copy-start | bytes 3145732
  151.4 3.7 %copy-start.10 = (bf16[4,512,256]{1,2,0:T(8,128)(2,1)S(1)}, bf16[4,512,256]{1,2,0:T(8,128)(2,1)}, u32[]{:S(2)}) copy-start(bf16[4,512,256]{1,2,0:T(8,128)(2,1)} %get-tuple-element.8) | copy-start | bytes 3145732
  162.5 48.3 %all-to-all-start.3 = ((bf16[1,4,512,128]{3,1,0,2:T(4,128)(2,1)}), bf16[1,4,512,128]{3,1,0,2:T(4,128)(2,1)S(1)}, u32[]{:S(2)}, u32[]{:S(2)}) async-start(bf16[1,4,512,128]{3,1,0,2:T(4,128)(2,1)} %copy.49), calls=%async_computation.3 | async-start | bytes 1048576 | tf_op jit(solution)/shard_map/all_to_all | solution.py:76
where the time goes:
time: 213 us; the launch traced here: 212 us
  other arithmetic  58.4 us (27%)
  waiting for transfers between devices  53.8 us (25%)
  starting transfers between devices  46 us (22%)
  matrix products  31 us (15%)
  local copies, waits for them, and re-layouts  21.9 us (10%)
    all_to_all x2, waiting for transfers between devices, per_device(): lax.all_to_all(formed[None], 'chan', split_axis=2, concat_axis=0, tiled=T...  32.6 us
    all_to_all x2, starting transfers between devices, per_device(): lax.all_to_all(formed[None], 'chan', split_axis=2, concat_axis=0, tiled=T...  30.3 us
    another operation x7, other arithmetic, power_step(): lower = jnp.linalg.cholesky(gram)  23.8 us
    all_to_all x2, waiting for transfers between devices, per_device(): lax.all_to_all(ordered[part], 'tm', split_axis=1, concat_axis=0, tiled=True)  21.2 us
    another operation x5, other arithmetic, power_step(): tracked = jax.scipy.linalg.solve_triangular(lower, beam_image, lower=True)  19.9 us
    all_to_all x2, starting transfers between devices, per_device(): lax.all_to_all(ordered[part], 'tm', split_axis=1, concat_axis=0, tiled=True)  15.8 us
    another operation x1, other arithmetic  9.12 us
    gather x1, local copies, waits for them, and re-layouts, per_device(): ordered = jnp.take(voltages, order, axis=2) * keep  7.92 us
  transfers between devices with their start and end apart: 4, of which 2 were waited for; matrix products, arithmetic and copies ran while one was open for 44% of the time, Pallas kernels for 0%

commit v1 on v0

--- a/solution.py
+++ b/solution.py
@@ -7,6 +7,18 @@
 CH = 2048
 SUB = 2
 TWO_PI = 2.0 * math.pi
+
+
+def pack_node_here(block_in):
+    return jnp.concatenate(
+        lax.all_to_all(
+            jnp.stack(jnp.split(block_in, lax.psum(1, axis_name="tm"), axis=1), axis=0),
+            axis_name="tm",
+            split_axis=0,
+            concat_axis=0,
+        ),
+        axis=0,
+    )
 
 
 def beam_weights(beam_seeds, channels, stations, total_channels):
@@ -70,7 +82,7 @@
     state = subspace[0]
     results = []
     for part in range(SUB):
-        turned = lax.all_to_all(ordered[part], "tm", split_axis=1, concat_axis=0, tiled=True)
+        turned = pack_node_here(ordered[part])
         state, formed = power_step(turned, state, steering_weight)
         results.append(
             lax.all_to_all(formed[None], "chan", split_axis=2, concat_axis=0, tiled=True)

time: 213 us -> 219 us (1.028)
  the two profiles are of different devices: /device:TPU:12 before, /device:TPU:18 now
where the time goes in v1:
time: 219 us; the launch traced here: 217 us
  other arithmetic  58.4 us (27%)
  local copies, waits for them, and re-layouts  50 us (23%)
  starting transfers between devices  46.6 us (21%)
  waiting for transfers between devices  32.6 us (15%)
  matrix products  29 us (13%)
    unnamed x54, local copies, waits for them, and re-layouts  33.8 us
    all_to_all x2, waiting for transfers between devices, per_device(): lax.all_to_all(formed[None], 'chan', split_axis=2, concat_axis=0, tiled=T...  32.6 us
    all_to_all x2, starting transfers between devices, per_device(): lax.all_to_all(formed[None], 'chan', split_axis=2, concat_axis=0, tiled=T...  30.2 us
    another operation x7, other arithmetic, power_step(): lower = jnp.linalg.cholesky(gram)  23.8 us
    another operation x5, other arithmetic, power_step(): tracked = jax.scipy.linalg.solve_triangular(lower, beam_image, lower=True)  19.9 us
    all_to_all x2, starting transfers between devices, pack_node_here(): lax.all_to_all(jnp.stack(jnp.split(block_in, lax.psum(1, axis_name='tm'),...  16.4 us
    another operation x1, other arithmetic  9.1 us
    gather x1, local copies, waits for them, and re-layouts, per_device(): ordered = jnp.take(voltages, order, axis=2) * keep  7.93 us
  transfers between devices with their start and end apart: 4, of which 1 were waited for; matrix products, arithmetic and copies ran while one was open for 51% of the time, Pallas kernels for 0%

profile of v1, /device:TPU:18, one launch (start us, length us, event | category | flops | bytes accessed | tf_op | source)
XLA Modules:
  0.0 217.5 jit_solution(1377130113008513899)
XLA Ops:
  2.9 7.9 %gather_fusion = bf16[64,2,8,1024]{3,0,2,1:T(8,128)(2,1)} fusion(bf16[2,8,64,1024]{3,2,1,0:T(8,128)(2,1)S(1)} %copy-done, s32[1024]{0:T(1024)S(1)} %pad_clamp_fusion), kind=kCustom, calls=%fused_computation | custom fusion | bytes 4194560 | tf_op jit(solution)/shard_map/jit(_take)/gather | solution.py:76
  10.8 1.8 multiply_bitcast_fusion
  24.3 8.9 %all-to-all-start = ((bf16[16,8,4,1024]{3,2,1,0:T(4,128)(2,1)}), bf16[16,8,4,1024]{3,2,1,0:T(4,128)(2,1)S(1)}, u32[]{:S(2)}, u32[]{:S(2)}) async-start(bf16[16,8,4,1024]{3,2,1,0:T(4,128)(2,1)} %fusion.60), calls=%async_computation | async-start | bytes 2097152 | tf_op jit(solution)/shard_map/all_to_all | solution.py:14
  34.7 1.6 fusion.58
  37.8 1.6 fusion.56
  40.9 1.6 fusion.54
  45.6 1.6 fusion.51
  47.1 1.6 fusion.50
  50.2 1.6 fusion.48
  53.3 1.6 fusion.46
  54.9 1.6 fusion.45
  56.4 1.6 fusion.44
  58.0 7.5 %all-to-all-start.2 = ((bf16[16,8,4,1024]{3,2,1,0:T(4,128)(2,1)}), bf16[16,8,4,1024]{3,2,1,0:T(4,128)(2,1)}, u32[]{:S(2)}, u32[]{:S(2)}) async-start(bf16[16,8,4,1024]{3,2,1,0:T(4,128)(2,1)} %fusion.44), calls=%async_computation.2 | async-start | bytes 2097152 | tf_op jit(solution)/shard_map/all_to_all | solution.py:14
  66.0 9.1 %fusion.4 = (bf16[4,512,256]{1,2,0:T(8,128)(2,1)}, bf16[4,512,256]{1,2,0:T(8,128)(2,1)}, bf16[4,512,256]{1,2,0:T(8,128)(2,1)}) fusion(f32[4]{0:T(128)S(1)} %add_multiply_fusion, f32[512,256]{0,1:T(8,128)S(1)} %fusion.33), kind=kLoop, calls=%fused_computation.8 | loop fusion | flops 3670016 | bytes 3670032 | tf_op jit(solution)/shard_map/convert.5
  75.1 3.1 %convolution_add_fusion.1 = f32[4,32,1024]{2,1,0:T(8,128)} fusion(bf16[16,8,4,1024]{3,2,1,0:T(4,128)(2,1)S(1)} %all-to-all-done, f32[1,4,32,1024]{3,2,1,0:T(8,128)} %param.9), kind=kOutput, calls=%fused_computation.18 | convolution fusion | flops 67518464 | bytes 2097152 | tf_op jit(solution)/shard_map/nwg,wny->ngy/dot_general | solution.py:44
  78.2 1.8 fusion.88
  80.2 11.7 %custom-call.8 = f32[4,32,32]{2,1,0:T(8,128)S(1)} custom-call(f32[4,32,32]{2,1,0:T(8,128)S(1)} %fusion.81), custom_call_target="Cholesky" | custom-call | tf_op jit(solution)/shard_map/jit(cholesky)/cholesky | solution.py:50
  92.1 9.8 %custom-call.9 = f32[4,1,32,32]{2,3,1,0:T(8,128)S(1)} custom-call(f32[4,1,32,32]{3,2,1,0:T(8,128)S(1)} %select_bitcast_fusion.1), custom_call_target="InvertDiagBlocksLowerTriangular" | custom-call | tf_op jit(solution)/shard_map/jit(_solve_triangular)/vmap()/triangular_solve | solution.py:51
  102.0 1.7 fusion.79
  104.5 3.7 %convolution_convert_fusion.1 = bf16[4,32,512]{2,1,0:T(8,128)(2,1)S(1)} fusion(f32[4,32,1024]{2,1,0:T(8,128)S(1)} %fusion.79, bf16[4,512,256]{1,2,0:T(8,128)(2,1)} %get-tuple-element.8, bf16[4,512,256]{1,2,0:T(8,128)(2,1)} %get-tuple-element.7, bf16[4,512,256]{1,2,0:T(8,128)(2,1)} %get-tuple-element.6), kind=kOutput, calls=%fused_computation.20 | convolution fusion | flops 151191552 | bytes 3801088 | tf_op jit(solution)/shard_map/crs,csb->crb/dot_general | solution.py:56
  108.2 2.4 %fusion.20 = f32[4,512,128]{2,1,0:T(8,128)} fusion(bf16[16,8,4,1024]{3,2,1,0:T(4,128)(2,1)S(1)} %all-to-all-done, bf16[4,512,256]{1,2,0:T(8,128)(2,1)S(1)} %copy-done.8, bf16[4,512,256]{1,2,0:T(8,128)(2,1)S(1)} %copy-done.6, bf16[4,512,256]{1,2,0:T(8,128)(2,1)S(1)} %copy-done.4), kind=kOutput, calls=%fused_computation.34 | convolution fusion | flops 553648128 | bytes 5242880 | tf_op jit(solution)/shard_map/edi,diy->dye/dot_general | solution.py:59
  110.6 2.9 %fusion.9 = bf16[1,4,512,128]{3,2,1,0:T(8,128)(2,1)} fusion(f32[4,512,128]{2,1,0:T(8,128)} %fusion.20, bf16[4,32,512]{2,1,0:T(8,128)(2,1)S(1)} %convolution_convert_fusion.1, bf16[16,8,4,1024]{3,2,1,0:T(4,128)(2,1)S(1)} %all-to-all-done, f32[4,32,1024]{2,1,0:T(8,128)} %copy-done.1), kind=kOutput, calls=%fused_computation.16 | convolution fusion | flops 51003392 | bytes 3276800 | tf_op jit(solution)/shard_map/ctr,crb->cbt/dot_general | solution.py:62
  113.5 2.3 %copy.39 = bf16[1,4,512,128]{3,1,0,2:T(4,128)(2,1)} copy(bf16[1,4,512,128]{3,2,1,0:T(8,128)(2,1)} %fusion.9) | data formatting | bytes 1048576 | tf_op jit(solution)/shard_map/broadcast_in_dim | solution.py:88
  115.8 15.6 %all-to-all-start.1 = ((bf16[1,4,512,128]{3,1,0,2:T(4,128)(2,1)}), bf16[1,4,512,128]{3,1,0,2:T(4,128)(2,1)}, u32[]{:S(2)}, u32[]{:S(2)}) async-start(bf16[1,4,512,128]{3,1,0,2:T(4,128)(2,1)} %copy.39), calls=%async_computation.1 | async-start | bytes 1048576 | tf_op jit(solution)/shard_map/all_to_all | solution.py:88
  131.4 2.6 %convolution_add_fusion = f32[4,32,1024]{2,1,0:T(8,128)S(1)} fusion(bf16[16,8,4,1024]{3,2,1,0:T(4,128)(2,1)} %all-to-all-done.2, f32[4,32,1024]{2,1,0:T(8,128)S(1)} %copy-done.2), kind=kOutput, calls=%fused_computation.17 | convolution fusion | flops 67518464 | bytes 2097152 | tf_op jit(solution)/shard_map/nwg,wny->ngy/dot_general | solution.py:44
  134.8 11.7 %custom-call.10 = f32[4,32,32]{2,1,0:T(8,128)S(1)} custom-call(f32[4,32,32]{2,1,0:T(8,128)S(1)} %fusion.78), custom_call_target="Cholesky" | custom-call | tf_op jit(solution)/shard_map/jit(cholesky)/cholesky | solution.py:50
  146.7 9.8 %custom-call.11 = f32[4,1,32,32]{2,3,1,0:T(8,128)S(1)} custom-call(f32[4,1,32,32]{3,2,1,0:T(8,128)S(1)} %select_bitcast_fusion), custom_call_target="InvertDiagBlocksLowerTriangular" | custom-call | tf_op jit(solution)/shard_map/jit(_solve_triangular)/vmap()/triangular_solve | solution.py:51
  157.3 3.7 %convolution_convert_fusion = bf16[4,32,512]{2,1,0:T(8,128)(2,1)S(1)} fusion(f32[4,32,1024]{2,1,0:T(8,128)S(1)} %fusion.76, bf16[4,512,256]{1,2,0:T(8,128)(2,1)} %get-tuple-element.8, bf16[4,512,256]{1,2,0:T(8,128)(2,1)} %get-tuple-element.7, bf16[4,512,256]{1,2,0:T(8,128)(2,1)} %get-tuple-element.6), kind=kOutput, calls=%fused_computation.19 | convolution fusion | flops 151191552 | bytes 3801088 | tf_op jit(solution)/shard_map/crs,csb->crb/dot_general | solution.py:56
  161.1 3.5 %fusion.14 = f32[4,512,128]{2,1,0:T(8,128)} fusion(bf16[16,8,4,1024]{3,2,1,0:T(4,128)(2,1)} %all-to-all-done.2, bf16[4,512,256]{1,2,0:T(8,128)(2,1)S(1)} %copy-done.9, bf16[4,512,256]{1,2,0:T(8,128)(2,1)S(1)} %copy-done.7, bf16[4,512,256]{1,2,0:T(8,128)(2,1)S(1)} %copy-done.5), kind=kOutput, calls=%fused_computation.30 | convolution fusion | flops 553648128 | bytes 5242880 | tf_op jit(solution)/shard_map/edi,diy->dye/dot_general | solution.py:59
  164.6 2.2 %fusion.8 = bf16[1,4,512,128]{3,2,1,0:T(8,128)(2,1)S(1)} fusion(f32[4,512,128]{2,1,0:T(8,128)} %fusion.14, bf16[4,32,512]{2,1,0:T(8,128)(2,1)S(1)} %convolution_convert_fusion, bf16[16,8,4,1024]{3,2,1,0:T(4,128)(2,1)} %all-to-all-done.2, f32[4,32,1024]{2,1,0:T(8,128)S(1)} %fusion.76), kind=kOutput, calls=%fused_computation.15 | convolution fusion | flops 51003392 | bytes 3276800 | tf_op jit(solution)/shard_map/ctr,crb->cbt/dot_general | solution.py:62
  168.0 14.6 %all-to-all-start.3 = ((bf16[1,4,512,128]{3,1,0,2:T(4,128)(2,1)}), bf16[1,4,512,128]{3,1,0,2:T(4,128)(2,1)S(1)}, u32[]{:S(2)}, u32[]{:S(2)}) async-start(bf16[1,4,512,128]{3,1,0,2:T(4,128)(2,1)} %copy.45), calls=%async_computation.3 | async-start | bytes 1048576 | tf_op jit(solution)/shard_map/all_to_all | solution.py:88
  183.7 32.6 %all-to-all-done.3 = bf16[1,4,512,128]{3,1,0,2:T(4,128)(2,1)S(1)} async-done(((bf16[1,4,512,128]{3,1,0,2:T(4,128)(2,1)}), bf16[1,4,512,128]{3,1,0,2:T(4,128)(2,1)S(1)}, u32[]{:S(2)}, u32[]{:S(2)}) %all-to-all-start.3) | async-done | bytes 524320 | tf_op jit(solution)/shard_map/all_to_all | solution.py:88
  (78 shorter events, 31.3 us)
Async XLA Ops:
  0.6 2.3 %copy-start = (bf16[2,8,64,1024]{3,2,1,0:T(8,128)(2,1)S(1)}, bf16[2,8,64,1024]{3,2,1,0:T(8,128)(2,1)}, u32[]{:S(2)}) copy-start(bf16[2,8,64,1024]{3,2,1,0:T(8,128)(2,1)} %param.8) | copy-start | bytes 6291460
  24.3 33.7 %all-to-all-start = ((bf16[16,8,4,1024]{3,2,1,0:T(4,128)(2,1)}), bf16[16,8,4,1024]{3,2,1,0:T(4,128)(2,1)S(1)}, u32[]{:S(2)}, u32[]{:S(2)}) async-start(bf16[16,8,4,1024]{3,2,1,0:T(4,128)(2,1)} %fusion.60), calls=%async_computation | async-start | bytes 2097152 | tf_op jit(solution)/shard_map/all_to_all | solution.py:14
  33.2 32.4 %copy-start.11 = (s32[64]{0:T(128)S(1)}, s32[64]{0:T(128)}, u32[]{:S(2)}) copy-start(s32[64]{0:T(128)} %param.10) | copy-start | bytes 772
  33.2 32.5 %copy-start.10 = (s32[256]{0:T(256)S(1)}, s32[256]{0:T(256)}, u32[]{:S(2)}) copy-start(s32[256]{0:T(256)} %param.11) | copy-start | bytes 3076
  58.0 57.8 %all-to-all-start.2 = ((bf16[16,8,4,1024]{3,2,1,0:T(4,128)(2,1)}), bf16[16,8,4,1024]{3,2,1,0:T(4,128)(2,1)}, u32[]{:S(2)}, u32[]{:S(2)}) async-start(bf16[16,8,4,1024]{3,2,1,0:T(4,128)(2,1)} %fusion.44), calls=%async_computation.2 | async-start | bytes 2097152 | tf_op jit(solution)/shard_map/all_to_all | solution.py:14
  103.7 0.8 copy-start.1
  104.5 3.7 %copy-start.4 = (bf16[4,512,256]{1,2,0:T(8,128)(2,1)S(1)}, bf16[4,512,256]{1,2,0:T(8,128)(2,1)}, u32[]{:S(2)}) copy-start(bf16[4,512,256]{1,2,0:T(8,128)(2,1)} %get-tuple-element.6) | copy-start | bytes 3145732
  104.5 3.7 %copy-start.6 = (bf16[4,512,256]{1,2,0:T(8,128)(2,1)S(1)}, bf16[4,512,256]{1,2,0:T(8,128)(2,1)}, u32[]{:S(2)}) copy-start(bf16[4,512,256]{1,2,0:T(8,128)(2,1)} %get-tuple-element.7) | copy-start | bytes 3145732
  104.5 3.7 %copy-start.8 = (bf16[4,512,256]{1,2,0:T(8,128)(2,1)S(1)}, bf16[4,512,256]{1,2,0:T(8,128)(2,1)}, u32[]{:S(2)}) copy-start(bf16[4,512,256]{1,2,0:T(8,128)(2,1)} %get-tuple-element.8) | copy-start | bytes 3145732
  113.5 17.9 %copy-start.2 = (f32[4,32,1024]{2,1,0:T(8,128)S(1)}, f32[4,32,1024]{2,1,0:T(8,128)}, u32[]{:S(2)}) copy-start(f32[4,32,1024]{2,1,0:T(8,128)} %copy-done.1) | copy-start | bytes 1572868
  115.8 52.2 %all-to-all-start.1 = ((bf16[1,4,512,128]{3,1,0,2:T(4,128)(2,1)}), bf16[1,4,512,128]{3,1,0,2:T(4,128)(2,1)}, u32[]{:S(2)}, u32[]{:S(2)}) async-start(bf16[1,4,512,128]{3,1,0,2:T(4,128)(2,1)} %copy.39), calls=%async_computation.1 | async-start | bytes 1048576 | tf_op jit(solution)/shard_map/all_to_all | solution.py:88
  157.3 7.3 %copy-start.3 = (f32[4,32,1024]{2,1,0:T(8,128)}, f32[4,32,1024]{2,1,0:T(8,128)S(1)}, u32[]{:S(2)}) copy-start(f32[4,32,1024]{2,1,0:T(8,128)S(1)} %fusion.76) | copy-start | bytes 1572868
  157.3 3.8 %copy-start.5 = (bf16[4,512,256]{1,2,0:T(8,128)(2,1)S(1)}, bf16[4,512,256]{1,2,0:T(8,128)(2,1)}, u32[]{:S(2)}) copy-start(bf16[4,512,256]{1,2,0:T(8,128)(2,1)} %get-tuple-element.6) | copy-start | bytes 3145732
  157.3 3.8 %copy-start.7 = (bf16[4,512,256]{1,2,0:T(8,128)(2,1)S(1)}, bf16[4,512,256]{1,2,0:T(8,128)(2,1)}, u32[]{:S(2)}) copy-start(bf16[4,512,256]{1,2,0:T(8,128)(2,1)} %get-tuple-element.7) | copy-start | bytes 3145732
  157.3 3.8 %copy-start.9 = (bf16[4,512,256]{1,2,0:T(8,128)(2,1)S(1)}, bf16[4,512,256]{1,2,0:T(8,128)(2,1)}, u32[]{:S(2)}) copy-start(bf16[4,512,256]{1,2,0:T(8,128)(2,1)} %get-tuple-element.8) | copy-start | bytes 3145732
  168.0 48.3 %all-to-all-start.3 = ((bf16[1,4,512,128]{3,1,0,2:T(4,128)(2,1)}), bf16[1,4,512,128]{3,1,0,2:T(4,128)(2,1)S(1)}, u32[]{:S(2)}, u32[]{:S(2)}) async-start(bf16[1,4,512,128]{3,1,0,2:T(4,128)(2,1)} %copy.45), calls=%async_computation.3 | async-start | bytes 1048576 | tf_op jit(solution)/shard_map/all_to_all | solution.py:88
